TPU v7x, 32 devices: a whole 2x2x4 slice. The times are simulated.
32 devices in a mesh: dp: 4 (over x, core), mp: 8 (over z, y).
Axes of the slice: x: 2, y: 2, z: 4, core: 2. Of those that a mesh axis runs over, the one named last changes fastest.
Arguments:
- attn_out: bfloat16 [512, 8192], P('dp', 'mp'), may hold values from -6 to 6
- residual: bfloat16 [512, 8192], P('dp', 'mp'), may hold values from -40 to 40
- output_weight: bfloat16 [8192, 8192], P('mp', 'dp'), may hold values from -0.0625 to 0.0625
- prune_mask: int32 [8192, 128], P('mp'), may hold values 0 or 1
- inverse_factor: float32 [128, 8192], P(None, 'dp'), may hold values from -2 to 2, as said below
- norm_gain: bfloat16 [8192], P('mp'), may hold values from 0.5 to 1.5
- gate_up_weight: bfloat16 [8192, 2, 14336], P('dp', None, 'mp'), may hold values from -0.0625 to 0.0625
Outputs:
- pruned_weight: bfloat16 [8192, 8192], P('mp', 'dp')
- stream: bfloat16 [512, 8192], P('dp', 'mp')
- hessian: float32 [14336, 14336], P('mp', 'dp')
Inputs may be any that keep to these rules, and one draw needn't show every extreme that they name: inverse_factor is zero below its diagonal, and its diagonal lies between 0.5 and 2.
All inputs are finite; a program needn't handle non-finite values. No bound on the sum of `prune_mask` on one device may be relied on, other than what follows from the above.
Results may differ from a plain program's by a relative error of at most 0.012.
Values may be sent and summed in bfloat16 or wider, within the bound.
A program may use at most 128 MiB of HBM per device.

v0:
```python
import jax
import jax.numpy as jnp
from jax import lax
from jax.sharding import PartitionSpec as P


def from_root(block, axis, holder):
    block = jnp.where(lax.axis_index(axis) == holder, block, jnp.zeros_like(block))
    return lax.psum(block, axis)


def body(attn_out, residual, output_weight, prune_mask, inverse_factor, norm_gain, gate_up_weight):
    width_block = prune_mask.shape[1]
    kept_mask = prune_mask.astype(jnp.float32)
    weight_cols = output_weight.astype(jnp.float32)
    is_first = lax.axis_index("dp") == 0
    factor_block = inverse_factor[:, :width_block]
    pivots = jnp.where(is_first, jnp.diagonal(factor_block), 1.0)
    cutting = (1.0 - kept_mask) / pivots[None, :]
    sub_width = min(32, width_block)
    strict = jnp.tril(jnp.ones((sub_width, sub_width), jnp.float32), -1)
    identity_sub = jnp.eye(sub_width, dtype=jnp.float32)[None, :, :]
    pieces = []
    for begin in range(0, width_block, sub_width):
        current = weight_cols[:, begin : begin + sub_width]
        if begin > 0:
            earlier = jnp.concatenate(pieces, axis=1)
            current = current - jnp.dot(
                earlier,
                factor_block[:begin, begin : begin + sub_width],
                precision=lax.Precision.HIGHEST,
                preferred_element_type=jnp.float32,
            )
        cut_part = cutting[:, begin : begin + sub_width]
        inner = factor_block[begin : begin + sub_width, begin : begin + sub_width]
        system = cut_part[:, :, None] * (inner.T * strict)[None, :, :] + identity_sub
        target = (cut_part * current)[:, :, None]
        pieces.append(
            jax.scipy.linalg.solve_triangular(system, target, lower=True, unit_diagonal=True)[
                :, :, 0
            ]
        )
    solved = jnp.concatenate(pieces, axis=1)
    errors = from_root(solved, "dp", 0)
    updated = weight_cols - jnp.dot(
        errors, inverse_factor, precision=lax.Precision.HIGHEST, preferred_element_type=jnp.float32
    )
    leading = jnp.where(is_first, updated[:, :width_block] * kept_mask, updated[:, :width_block])
    pruned_weight = lax.dynamic_update_slice_in_dim(updated, leading, 0, 1).astype(jnp.bfloat16)
    features = lax.all_gather(attn_out, "mp", axis=1, tiled=True)
    projected = lax.dot_general(
        features,
        lax.all_gather(pruned_weight, "dp", axis=1, tiled=True),
        (((1,), (1,)), ((), ())),
        preferred_element_type=jnp.float32,
    )
    stream = (residual.astype(jnp.float32) + projected).astype(jnp.bfloat16)
    width_model = features.shape[1]
    stream_float = stream.astype(jnp.float32)
    squares = lax.psum(jnp.sum(stream_float * stream_float, axis=1), "mp")
    inverse = lax.rsqrt(squares / width_model + 1e-05)
    normed = (stream_float * inverse[:, None] * norm_gain.astype(jnp.float32)[None, :]).astype(
        jnp.bfloat16
    )
    normed_all = lax.all_gather(normed, "mp", axis=1, tiled=True)
    input_rows = gate_up_weight.shape[0]
    unit_count = gate_up_weight.shape[2]
    slices = lax.all_to_all(normed_all, "dp", split_axis=1, concat_axis=0, tiled=True)
    flat_weight = gate_up_weight.reshape(input_rows, 2 * unit_count)
    gate_up = lax.psum_scatter(
        jnp.dot(slices, flat_weight, preferred_element_type=jnp.float32),
        "dp",
        scatter_dimension=0,
        tiled=True,
    )
    gate_part = gate_up[:, :unit_count]
    up_part = gate_up[:, unit_count:]
    hidden = (jax.nn.silu(gate_part) * up_part).astype(jnp.bfloat16)
    hidden_all = lax.all_gather(hidden, "mp", axis=1, tiled=True)
    count_rows = hidden_all.shape[1] // lax.axis_size("mp")
    window_local = lax.dynamic_slice_in_dim(
        hidden_all, lax.axis_index("mp") * count_rows, count_rows, 1
    )
    weighting = 2.0 / (hidden_all.shape[0] * lax.axis_size("dp"))
    contract = (((0,), (0,)), ((), ()))
    columns = lax.all_to_all(hidden_all, "dp", split_axis=1, concat_axis=0, tiled=True)
    window_all = lax.all_gather(window_local, "dp", axis=0, tiled=True)
    hessian = weighting * lax.dot_general(
        window_all, columns, contract, preferred_element_type=jnp.float32
    )
    return (pruned_weight, stream, hessian)


def solution(mesh):
    in_specs = (
        P("dp", "mp"),
        P("dp", "mp"),
        P("mp", "dp"),
        P("mp", None),
        P(None, "dp"),
        P("mp"),
        P("dp", None, "mp"),
    )
    out_specs = (P("mp", "dp"), P("dp", "mp"), P("mp", "dp"))
    return jax.shard_map(body, mesh=mesh, in_specs=in_specs, out_specs=out_specs, check_vma=False)
```

profile of v0, /device:TPU:0, one launch (start us, length us, event | category | flops | bytes accessed | tf_op | source)
XLA Modules:
  0.0 952.4 jit_solution(11305181622557403256)
XLA Ops:
  8.0 0.0 all-reduce.2.cloned.1.call-start
  8.1 0.9 select_multiply_fusion.3
  8.9 0.1 iota_compare_fusion.1
  9.0 1.2 copy.21
  10.3 6.4 copy.20
  16.7 6.7 convert_element_type.40
  23.3 0.1 copy.22
  23.4 0.1 copy.23
  23.5 0.1 copy.24
  23.5 0.1 copy.25
  23.6 1.3 gather_fusion
  24.9 0.1 subtract_divide_fusion
  25.0 1.0 slice_multiply_fusion.1
  26.0 7.3 add_bitcast_fusion.3
  33.3 100.7 %custom-call.8 = f32[1024,1,32,32]{0,2,3,1:T(8,128)} custom-call(f32[1024,1,32,32]{0,3,2,1:T(8,128)} %get-tuple-element.19), custom_call_target="InvertDiagBlocksLowerTriangular" | custom-call | tf_op jit(solution)/shard_map/jit(_solve_triangular)/vmap()/triangular_solve | solution.py:39
  134.0 2.7 fusion.3
  136.7 1.3 fusion.7
  138.0 100.7 %custom-call.9 = f32[1024,1,32,32]{0,2,3,1:T(8,128)} custom-call(f32[1024,1,32,32]{0,3,2,1:T(8,128)} %get-tuple-element.20), custom_call_target="InvertDiagBlocksLowerTriangular" | custom-call | tf_op jit(solution)/shard_map/jit(_solve_triangular)/vmap()/triangular_solve | solution.py:39
  238.7 2.7 fusion.2
  241.4 1.3 fusion.8
  242.7 100.6 %custom-call.10 = f32[1024,1,32,32]{0,2,3,1:T(8,128)} custom-call(f32[1024,1,32,32]{0,3,2,1:T(8,128)} %get-tuple-element.21), custom_call_target="InvertDiagBlocksLowerTriangular" | custom-call | tf_op jit(solution)/shard_map/jit(_solve_triangular)/vmap()/triangular_solve | solution.py:39
  343.3 2.7 fusion.1
  346.0 1.3 fusion.6
  347.4 100.6 %custom-call.11 = f32[1024,1,32,32]{0,2,3,1:T(8,128)} custom-call(f32[1024,1,32,32]{0,3,2,1:T(8,128)} %get-tuple-element.22), custom_call_target="InvertDiagBlocksLowerTriangular" | custom-call | tf_op jit(solution)/shard_map/jit(_solve_triangular)/vmap()/triangular_solve | solution.py:39
  448.0 2.7 fusion
  450.7 0.8 maximum_select_fusion
  451.5 0.0 all-reduce.2.cloned.1.call-update
  451.5 0.0 all-gather.8.cloned.1.call-start
  451.6 0.5 all-gather.8.cloned.1.call-update
  452.1 0.2 all-gather.6.cloned.1.call-start
  452.4 35.5 %all-reduce.2.cloned.1.call-done = f32[1024,128]{0,1:T(8,128)} async-done(((f32[1024,128]{0,1:T(8,128)}), f32[1024,128]{0,1:T(8,128)}) %all-reduce.2.cloned.1.call-update) | async-done | bytes 524304 | tf_op jit(solution)/shard_map/psum | solution.py:9
  487.8 12.2 %convolution_subtract_fusion = f32[1024,2048]{0,1:T(8,128)S(1)} fusion(f32[1024,128]{0,1:T(8,128)} %all-reduce.2.cloned.1.call-done, f32[128,2048]{1,0:T(8,128)S(1)} %copy-done, bf16[1024,2048]{0,1:T(8,128)(2,1)} %copy.20), kind=kOutput, calls=%fused_computation.2 | convolution fusion | flops 3225419776 | bytes 14155776 | tf_op jit(solution)/shard_map/dot_general | solution.py:45
  500.0 0.2 fusion.13
  500.2 2.6 convert_element_type.43
  502.8 0.0 all-gather.6.cloned.1.call-update
  502.9 0.0 all-gather.10.cloned.1.call-start
  502.9 0.9 copy-done.1
  503.8 0.2 copy.27
  504.0 1.9 all-gather.8.cloned.1.call-done
  505.9 105.8 %all-gather.6.cloned.1.call-done = bf16[1024,8192]{0,1:T(8,128)(2,1)} async-done(((bf16[1024,2048]{0,1:T(8,128)(2,1)}), bf16[1024,8192]{0,1:T(8,128)(2,1)}) %all-gather.6.cloned.1.call-update) | async-done | bytes 16777232 | tf_op jit(solution)/shard_map/all_gather | solution.py:53
  611.7 10.9 %fusion.10 = (f32[128]{0:T(128)S(1)}, bf16[128,1024]{0,1:T(8,128)(2,1)S(1)}) fusion(bf16[1024,8192]{0,1:T(8,128)(2,1)} %all-gather.6.cloned.1.call-done, bf16[128,8192]{1,0:T(8,128)(2,1)} %all-gather.8.cloned.1.call-done, bf16[128,1024]{0,1:T(8,128)(2,1)S(1)} %copy.27), kind=kOutput, calls=%fused_computation.30 | convolution fusion | flops 2148270080 | bytes 19399168 | tf_op jit(solution)/shard_map/dot_general | solution.py:51
  622.7 21.4 %psum.15 = f32[128]{0:T(128)S(1)} all-reduce(f32[128]{0:T(128)S(1)} %get-tuple-element.23), channel_id=1, replica_groups=mesh['dp'=4,'mp'=8] {'mp'}, use_global_device_ids=true, to_apply=%region_2.4 | all-reduce | flops 128 | bytes 1024 | tf_op jit(solution)/shard_map/psum | solution.py:60
  644.0 0.9 fusion.12
  645.0 0.0 all-gather.10.cloned.1.call-update
  645.0 45.4 %all-gather.10.cloned.1.call-done = bf16[128,8192]{0,1:T(8,128)(2,1)} async-done(((bf16[128,1024]{0,1:T(8,128)(2,1)}), bf16[128,8192]{0,1:T(8,128)(2,1)}) %all-gather.10.cloned.1.call-update) | async-done | bytes 2097168 | tf_op jit(solution)/shard_map/all_gather | solution.py:65
  690.4 3.9 copy.28
  694.3 3.6 all-to-all-start
  697.9 0.3 reduce-scatter.2.cloned.1.call-start
  698.2 16.0 %copy.58 = bf16[256,8,2,1792]{3,1,2,0:T(8,128)(2,1)} copy(bf16[256,8,2,1792]{3,2,1,0:T(2,128)(2,1)} %bitcast.78) | data formatting | bytes 29360128
  714.2 9.3 all-to-all-done
  723.6 12.9 %fusion.29 = f32[512,3584]{1,0:T(8,128)} fusion(bf16[512,2048]{1,0:T(8,128)(2,1)S(1)} %bitcast.82, bf16[2048,3584]{1,0:T(8,128)(2,1)} %bitcast.79), kind=kOutput, calls=%fused_computation.65 | convolution fusion | flops 7516192768 | bytes 24117248 | tf_op jit(solution)/shard_map/dot_general | solution.py:71
  736.5 0.0 all-gather.12.cloned.1.call-start
  736.5 63.7 %reduce-scatter.2.cloned.1.call-done = f32[128,3584]{1,0:T(8,128)} async-done(((f32[512,3584]{1,0:T(8,128)}), f32[128,3584]{1,0:T(8,128)}) %reduce-scatter.2.cloned.1.call-update) | async-done | bytes 1835024 | tf_op jit(solution)/shard_map/reduce_scatter | solution.py:70
  800.3 2.5 fusion.9
  802.7 0.0 all-gather.12.cloned.1.call-update
  802.8 66.2 %all-gather.12.cloned.1.call-done = bf16[128,14336]{1,0:T(8,128)(2,1)} async-done(((bf16[128,1792]{1,0:T(8,128)(2,1)}), bf16[128,14336]{1,0:T(8,128)(2,1)}) %all-gather.12.cloned.1.call-update) | async-done | bytes 3670032 | tf_op jit(solution)/shard_map/all_gather | solution.py:79
  869.0 4.2 copy.60
  873.2 4.7 all-to-all-start.1
  877.9 0.0 all-gather.14.cloned.1.call-start
  878.0 1.8 constant_dynamic-slice_fusion
  879.8 6.4 copy.30
  886.2 0.8 copy.31
  887.1 43.2 %all-to-all-done.1 = bf16[128,4,3584]{2,0,1:T(8,128)(2,1)} async-done(((bf16[128,4,3584]{2,0,1:T(8,128)(2,1)}), bf16[128,4,3584]{2,0,1:T(8,128)(2,1)}, u32[]{:S(2)}, u32[]{:S(2)}) %all-to-all-start.1) | async-done | bytes 3670048 | tf_op jit(solution)/shard_map/all_to_all | solution.py:86
  930.3 14.7 %convolution_multiply_fusion = f32[1792,3584]{1,0:T(8,128)} fusion(bf16[512,1792]{1,0:T(8,128)(2,1)} %all-gather.14.cloned.1.call-done, bf16[512,3584]{1,0:T(8,128)(2,1)} %bitcast.34), kind=kOutput, calls=%fused_computation.1 | convolution fusion | flops 6583091200 | bytes 31195136 | tf_op jit(solution)/shard_map/dot_general | solution.py:88
  (16 shorter events, 0.1 us)
Async XLA Ops:
  8.0 479.9 %all-reduce.2.cloned.1.call-start = ((), (), s32[]{:S(2)}) async-start(), calls=%async_computation.3 | async-start | bytes 1048576 | tf_op jit(solution)/shard_map/psum | solution.py:9
  16.7 7.0 slice-start
  33.2 103.4 %copy-start = (f32[128,2048]{1,0:T(8,128)S(1)}, f32[128,2048]{1,0:T(8,128)}, u32[]{:S(2)}) copy-start(f32[128,2048]{1,0:T(8,128)} %param.13) | copy-start | bytes 3145732
  451.5 54.4 %all-gather.8.cloned.1.call-start = ((), (), s32[]{:S(2)}) async-start(), calls=%async_computation.5 | async-start | bytes 2359296 | tf_op jit(solution)/shard_map/all_gather | solution.py:50
  452.1 159.6 %all-gather.6.cloned.1.call-start = ((), (), s32[]{:S(2)}) async-start(), calls=%async_computation.4 | async-start | bytes 20971520 | tf_op jit(solution)/shard_map/all_gather | solution.py:53
  502.8 0.9 copy-start.1
  502.8 1.1 copy-start.2
  502.9 187.5 %all-gather.10.cloned.1.call-start = ((), (), s32[]{:S(2)}) async-start(), calls=%async_computation.6 | async-start | bytes 2359296 | tf_op jit(solution)/shard_map/all_gather | solution.py:65
  694.3 29.2 %all-to-all-start = ((bf16[128,4,2048]{2,0,1:T(8,128)(2,1)}), bf16[128,4,2048]{2,0,1:T(8,128)(2,1)S(1)}, u32[]{:S(2)}, u32[]{:S(2)}) async-start(bf16[128,4,2048]{2,0,1:T(8,128)(2,1)} %copy.28), calls=%async_computation | async-start | bytes 4194304 | tf_op jit(solution)/shard_map/all_to_all | solution.py:68
  697.9 102.3 %reduce-scatter.2.cloned.1.call-start = ((), (), s32[]{:S(2)}) async-start(), calls=%async_computation.7 | async-start | bytes 9175040 | tf_op jit(solution)/shard_map/reduce_scatter | solution.py:70
  736.5 132.5 %all-gather.12.cloned.1.call-start = ((), (), s32[]{:S(2)}) async-start(), calls=%async_computation.8 | async-start | bytes 4128768 | tf_op jit(solution)/shard_map/all_gather | solution.py:79
  873.2 57.2 %all-to-all-start.1 = ((bf16[128,4,3584]{2,0,1:T(8,128)(2,1)}), bf16[128,4,3584]{2,0,1:T(8,128)(2,1)}, u32[]{:S(2)}, u32[]{:S(2)}) async-start(bf16[128,4,3584]{2,0,1:T(8,128)(2,1)} %bitcast.80), calls=%async_computation.2 | async-start | bytes 7340032 | tf_op jit(solution)/shard_map/all_to_all | solution.py:86
  877.9 52.4 %all-gather.14.cloned.1.call-start = ((), (), s32[]{:S(2)}) async-start(), calls=%async_computation.9 | async-start | bytes 2293760 | tf_op jit(solution)/shard_map/all_gather | solution.py:87
Sparse Core Ops, SparseCore 0:
  451.7 36.1 all-reduce.1
  736.6 63.6 reduce-scatter.1
  880.3 30.1 all-gather.13
Sparse Core Ops, SparseCore 1:
  454.2 51.6 all-gather.7
  507.3 104.3 all-gather.5
  645.1 45.3 all-gather.9
  802.9 66.1 all-gather.11
where the time goes:
time: 954 us; the launch traced here: 952 us
  other arithmetic  437 us (46%)
  waiting for transfers between devices  372 us (39%)
  matrix products  54.6 us (6%)
  local copies, waits for them, and re-layouts  43.5 us (5%)
  blocking collectives  21.4 us (2%)
  between operations  15.6 us (2%)
    another operation x12, other arithmetic, body(): jax.scipy.linalg.solve_triangular(system, target, lower=True, unit_diagon...  421 us
    all_gather x1, waiting for transfers between devices, body(): lax.all_gather(pruned_weight, 'dp', axis=1, tiled=True)  106 us
    all_gather x1, waiting for transfers between devices, body(): hidden_all = lax.all_gather(hidden, 'mp', axis=1, tiled=True)  66.2 us
    reduce_scatter x1, waiting for transfers between devices, body(): lax.psum_scatter(jnp.dot(slices, flat_weight, preferred_element_type=jnp....  63.7 us
    all_gather x1, waiting for transfers between devices, body(): normed_all = lax.all_gather(normed, 'mp', axis=1, tiled=True)  45.4 us
    all_to_all x1, waiting for transfers between devices, body(): lax.all_to_all(hidden_all, 'dp', split_axis=1, concat_axis=0, tiled=True)  43.2 us
    psum x1, waiting for transfers between devices, from_root(): return lax.psum(block, axis)  35.5 us
    unnamed x12, local copies, waits for them, and re-layouts  32 us
  transfers between devices with their start and end apart: 9, of which 8 were waited for; matrix products, arithmetic and copies ran while one was open for 4% of the time, Pallas kernels for 0%

commit v1 on v0

--- a/solution.py
+++ b/solution.py
@@ -76,7 +76,12 @@
     gate_part = gate_up[:, :unit_count]
     up_part = gate_up[:, unit_count:]
     hidden = (jax.nn.silu(gate_part) * up_part).astype(jnp.bfloat16)
-    hidden_all = lax.all_gather(hidden, "mp", axis=1, tiled=True)
+    ring = [hidden]
+    for hop in range(7):
+        ring.append(lax.ppermute(ring[-1], "mp", [(dev, (dev + 1) % 8) for dev in range(8)]))
+    hidden_all = jnp.roll(
+        jnp.concatenate(ring[::-1], axis=1), (lax.axis_index("mp") + 1) * ring[0].shape[1], axis=1
+    )
     count_rows = hidden_all.shape[1] // lax.axis_size("mp")
     window_local = lax.dynamic_slice_in_dim(
         hidden_all, lax.axis_index("mp") * count_rows, count_rows, 1

time: 954 us -> 998 us (1.046)
  local copies, waits for them, and re-layouts: 43.5 us -> 65.9 us
  waiting for transfers between devices: 372 us -> 392 us
    ppermute x0 -> x7, waiting for transfers between devices: none -> 86.9 us  [body(): lax.ppermute(ring[-1], 'mp', [(dev, (dev + 1) % 8) for dev in range(8)])]
    all_gather x1 -> x0, waiting for transfers between devices: 66.2 us -> none  [body(): hidden_all = lax.all_gather(hidden, 'mp', axis=1, tiled=True)]
    unnamed x12 -> x38, local copies, waits for them, and re-layouts: 32 us -> 43.4 us
  transfers between devices with their start and end apart: 9 -> 15, of which waited for: 8 -> 14; matrix products, arithmetic and copies ran while one was open for 4% -> 5% of each run, Pallas kernels for 0% -> 0%
where the time goes in v1:
time: 998 us; the launch traced here: 997 us
  other arithmetic  436 us (44%)
  waiting for transfers between devices  392 us (39%)
  local copies, waits for them, and re-layouts  65.9 us (7%)
  matrix products  54.6 us (5%)
  blocking collectives  21.4 us (2%)
  between operations  15.8 us (2%)
  starting transfers between devices  10.8 us (1%)
    another operation x12, other arithmetic, body(): jax.scipy.linalg.solve_triangular(system, target, lower=True, unit_diagon...  421 us
    all_gather x1, waiting for transfers between devices, body(): lax.all_gather(pruned_weight, 'dp', axis=1, tiled=True)  106 us
    ppermute x7, waiting for transfers between devices, body(): lax.ppermute(ring[-1], 'mp', [(dev, (dev + 1) % 8) for dev in range(8)])  86.9 us
    reduce_scatter x1, waiting for transfers between devices, body(): lax.psum_scatter(jnp.dot(slices, flat_weight, preferred_element_type=jnp....  63.8 us
    all_gather x1, waiting for transfers between devices, body(): normed_all = lax.all_gather(normed, 'mp', axis=1, tiled=True)  45.4 us
    unnamed x38, local copies, waits for them, and re-layouts  43.4 us
    all_to_all x1, waiting for transfers between devices, body(): lax.all_to_all(hidden_all, 'dp', split_axis=1, concat_axis=0, tiled=True)  42.8 us
    psum x1, waiting for transfers between devices, from_root(): return lax.psum(block, axis)  35.5 us
  transfers between devices with their start and end apart: 15, of which 14 were waited for; matrix products, arithmetic and copies ran while one was open for 5% of the time, Pallas kernels for 0%

profile of v1, /device:TPU:0, one launch (start us, length us, event | category | flops | bytes accessed | tf_op | source)
XLA Modules:
  0.0 996.8 jit_solution(11041552243087155822)
XLA Ops:
  8.1 0.9 select_multiply_fusion.3
  9.0 1.2 copy.32
  10.3 6.4 copy.31
  16.7 6.7 convert_element_type.40
  23.6 1.3 gather_fusion
  25.0 1.0 slice_multiply_fusion.1
  26.0 7.2 add_bitcast_fusion.3
  33.2 100.7 %custom-call.8 = f32[1024,1,32,32]{0,2,3,1:T(8,128)} custom-call(f32[1024,1,32,32]{0,3,2,1:T(8,128)} %get-tuple-element.22), custom_call_target="InvertDiagBlocksLowerTriangular" | custom-call | tf_op jit(solution)/shard_map/jit(_solve_triangular)/vmap()/triangular_solve | solution.py:39
  133.9 2.7 fusion.3
  136.7 1.3 fusion.7
  137.9 100.7 %custom-call.9 = f32[1024,1,32,32]{0,2,3,1:T(8,128)} custom-call(f32[1024,1,32,32]{0,3,2,1:T(8,128)} %get-tuple-element.23), custom_call_target="InvertDiagBlocksLowerTriangular" | custom-call | tf_op jit(solution)/shard_map/jit(_solve_triangular)/vmap()/triangular_solve | solution.py:39
  238.6 2.7 fusion.2
  241.3 1.3 fusion.8
  242.6 100.6 %custom-call.10 = f32[1024,1,32,32]{0,2,3,1:T(8,128)} custom-call(f32[1024,1,32,32]{0,3,2,1:T(8,128)} %get-tuple-element.24), custom_call_target="InvertDiagBlocksLowerTriangular" | custom-call | tf_op jit(solution)/shard_map/jit(_solve_triangular)/vmap()/triangular_solve | solution.py:39
  343.2 2.7 fusion.1
  346.0 1.3 fusion.6
  347.3 100.6 %custom-call.11 = f32[1024,1,32,32]{0,2,3,1:T(8,128)} custom-call(f32[1024,1,32,32]{0,3,2,1:T(8,128)} %get-tuple-element.25), custom_call_target="InvertDiagBlocksLowerTriangular" | custom-call | tf_op jit(solution)/shard_map/jit(_solve_triangular)/vmap()/triangular_solve | solution.py:39
  447.9 2.7 fusion
  450.6 0.8 maximum_select_fusion
  451.5 0.5 all-gather.7.cloned.1.call-update
  452.3 35.5 %all-reduce.2.cloned.1.call-done = f32[1024,128]{0,1:T(8,128)} async-done(((f32[1024,128]{0,1:T(8,128)}), f32[1024,128]{0,1:T(8,128)}) %all-reduce.2.cloned.1.call-update) | async-done | bytes 524304 | tf_op jit(solution)/shard_map/psum | solution.py:9
  487.8 12.2 %convolution_subtract_fusion = f32[1024,2048]{0,1:T(8,128)S(1)} fusion(f32[1024,128]{0,1:T(8,128)} %all-reduce.2.cloned.1.call-done, f32[128,2048]{1,0:T(8,128)S(1)} %copy-done.1, bf16[1024,2048]{0,1:T(8,128)(2,1)} %copy.31), kind=kOutput, calls=%fused_computation.2 | convolution fusion | flops 3225419776 | bytes 14155776 | tf_op jit(solution)/shard_map/dot_general | solution.py:45
  500.2 2.6 convert_element_type.43
  502.9 0.9 copy-done.7
  503.9 1.9 all-gather.7.cloned.1.call-done
  505.8 105.8 %all-gather.5.cloned.1.call-done = bf16[1024,8192]{0,1:T(8,128)(2,1)} async-done(((bf16[1024,2048]{0,1:T(8,128)(2,1)}), bf16[1024,8192]{0,1:T(8,128)(2,1)}) %all-gather.5.cloned.1.call-update) | async-done | bytes 16777232 | tf_op jit(solution)/shard_map/all_gather | solution.py:53
  611.7 10.9 %fusion.10 = (f32[128]{0:T(128)S(1)}, bf16[128,1024]{0,1:T(8,128)(2,1)S(1)}) fusion(bf16[1024,8192]{0,1:T(8,128)(2,1)} %all-gather.5.cloned.1.call-done, bf16[128,8192]{1,0:T(8,128)(2,1)} %all-gather.7.cloned.1.call-done, bf16[128,1024]{0,1:T(8,128)(2,1)S(1)} %copy.38), kind=kOutput, calls=%fused_computation.29 | convolution fusion | flops 2148270080 | bytes 19399168 | tf_op jit(solution)/shard_map/dot_general | solution.py:51
  622.6 21.4 %psum.15 = f32[128]{0:T(128)S(1)} all-reduce(f32[128]{0:T(128)S(1)} %get-tuple-element.26), channel_id=1, replica_groups=mesh['dp'=4,'mp'=8] {'mp'}, use_global_device_ids=true, to_apply=%region_2.4 | all-reduce | flops 128 | bytes 1024 | tf_op jit(solution)/shard_map/psum | solution.py:60
  644.0 0.9 fusion.12
  644.9 45.4 %all-gather.9.cloned.1.call-done = bf16[128,8192]{0,1:T(8,128)(2,1)} async-done(((bf16[128,1024]{0,1:T(8,128)(2,1)}), bf16[128,8192]{0,1:T(8,128)(2,1)}) %all-gather.9.cloned.1.call-update) | async-done | bytes 2097168 | tf_op jit(solution)/shard_map/all_gather | solution.py:65
  690.3 3.9 copy.39
  694.2 3.6 all-to-all-start
  698.1 16.0 %copy.69 = bf16[256,8,2,1792]{3,1,2,0:T(8,128)(2,1)} copy(bf16[256,8,2,1792]{3,2,1,0:T(2,128)(2,1)} %bitcast.74) | data formatting | bytes 29360128
  714.2 9.3 all-to-all-done
  723.5 12.9 %fusion.29 = f32[512,3584]{1,0:T(8,128)} fusion(bf16[512,2048]{1,0:T(8,128)(2,1)S(1)} %bitcast.78, bf16[2048,3584]{1,0:T(8,128)(2,1)} %bitcast.75), kind=kOutput, calls=%fused_computation.81 | convolution fusion | flops 7516192768 | bytes 24117248 | tf_op jit(solution)/shard_map/dot_general | solution.py:71
  736.4 63.8 %reduce-scatter.2.cloned.1.call-done = f32[128,3584]{1,0:T(8,128)} async-done(((f32[512,3584]{1,0:T(8,128)}), f32[128,3584]{1,0:T(8,128)}) %reduce-scatter.2.cloned.1.call-update) | async-done | bytes 1835024 | tf_op jit(solution)/shard_map/reduce_scatter | solution.py:70
  800.2 1.8 fusion.9
  802.1 1.6 collective-permute-start
  803.6 13.3 %collective-permute-done = bf16[128,1792]{1,0:T(8,128)(2,1)S(1)} collective-permute-done((bf16[128,1792]{1,0:T(8,128)(2,1)S(1)}, bf16[128,1792]{1,0:T(8,128)(2,1)S(1)}, u32[]{:S(2)}, u32[]{:S(2)}) %collective-permute-start) | collective-permute-done | bytes 458784 | tf_op jit(solution)/shard_map/ppermute | solution.py:81
  816.9 13.9 %collective-permute-done.1 = bf16[128,1792]{1,0:T(8,128)(2,1)S(1)} collective-permute-done((bf16[128,1792]{1,0:T(8,128)(2,1)S(1)}, bf16[128,1792]{1,0:T(8,128)(2,1)S(1)}, u32[]{:S(2)}, u32[]{:S(2)}) %collective-permute-start.1) | collective-permute-done | bytes 458784 | tf_op jit(solution)/shard_map/ppermute | solution.py:81
  830.9 13.1 %collective-permute-done.2 = bf16[128,1792]{1,0:T(8,128)(2,1)S(1)} collective-permute-done((bf16[128,1792]{1,0:T(8,128)(2,1)S(1)}, bf16[128,1792]{1,0:T(8,128)(2,1)S(1)}, u32[]{:S(2)}, u32[]{:S(2)}) %collective-permute-start.2) | collective-permute-done | bytes 458784 | tf_op jit(solution)/shard_map/ppermute | solution.py:81
  844.0 12.2 %collective-permute-done.3 = bf16[128,1792]{1,0:T(8,128)(2,1)S(1)} collective-permute-done((bf16[128,1792]{1,0:T(8,128)(2,1)S(1)}, bf16[128,1792]{1,0:T(8,128)(2,1)S(1)}, u32[]{:S(2)}, u32[]{:S(2)}) %collective-permute-start.3) | collective-permute-done | bytes 458784 | tf_op jit(solution)/shard_map/ppermute | solution.py:81
  856.2 0.8 copy-done.3
  857.0 11.4 %collective-permute-done.4 = bf16[128,1792]{1,0:T(8,128)(2,1)S(1)} collective-permute-done((bf16[128,1792]{1,0:T(8,128)(2,1)S(1)}, bf16[128,1792]{1,0:T(8,128)(2,1)S(1)}, u32[]{:S(2)}, u32[]{:S(2)}) %collective-permute-start.4) | collective-permute-done | bytes 458784 | tf_op jit(solution)/shard_map/ppermute | solution.py:81
  868.3 0.8 copy-done.5
  869.1 11.4 %collective-permute-done.5 = bf16[128,1792]{1,0:T(8,128)(2,1)} collective-permute-done((bf16[128,1792]{1,0:T(8,128)(2,1)S(1)}, bf16[128,1792]{1,0:T(8,128)(2,1)}, u32[]{:S(2)}, u32[]{:S(2)}) %collective-permute-start.5) | collective-permute-done | bytes 458784 | tf_op jit(solution)/shard_map/ppermute | solution.py:81
  880.5 11.5 %collective-permute-done.6 = bf16[128,1792]{1,0:T(8,128)(2,1)} collective-permute-done((bf16[128,1792]{1,0:T(8,128)(2,1)}, bf16[128,1792]{1,0:T(8,128)(2,1)}, u32[]{:S(2)}, u32[]{:S(2)}) %collective-permute-start.6) | collective-permute-done | bytes 458784 | tf_op jit(solution)/shard_map/ppermute | solution.py:81
  892.0 1.1 constant_dynamic-update-slice_fusion.15
  893.1 1.1 constant_dynamic-update-slice_fusion.14
  894.2 1.1 constant_dynamic-update-slice_fusion.13
  895.3 1.1 constant_dynamic-update-slice_fusion.12
  896.8 1.1 constant_dynamic-update-slice_fusion.7
  897.9 1.1 constant_dynamic-update-slice_fusion.6
  899.5 3.0 copy-done.2
  902.5 3.0 constant_dynamic-slice_fusion
  905.5 6.0 copy.40
  911.6 4.7 all-to-all-start.1
  916.3 0.3 all-gather.11.cloned.1.call-start
  916.6 2.0 constant_dynamic-slice_fusion.1
  918.6 6.5 copy.42
  925.1 0.8 copy.43
  926.0 42.8 %all-to-all-done.1 = bf16[128,4,3584]{0,2,1:T(8,128)(2,1)} async-done(((bf16[128,4,3584]{0,2,1:T(8,128)(2,1)}), bf16[128,4,3584]{0,2,1:T(8,128)(2,1)}, u32[]{:S(2)}, u32[]{:S(2)}) %all-to-all-start.1) | async-done | bytes 3670048 | tf_op jit(solution)/shard_map/all_to_all | solution.py:91
  968.7 6.0 copy.41
  974.7 14.7 %convolution_multiply_fusion = f32[1792,3584]{1,0:T(8,128)} fusion(bf16[512,1792]{1,0:T(8,128)(2,1)} %all-gather.11.cloned.1.call-done, bf16[512,3584]{1,0:T(8,128)(2,1)} %bitcast.77), kind=kOutput, calls=%fused_computation.1 | convolution fusion | flops 6583091200 | bytes 31195136 | tf_op jit(solution)/shard_map/dot_general | solution.py:93
  (57 shorter events, 2.5 us)
Async XLA Ops:
  8.0 479.8 %all-reduce.2.cloned.1.call-start = ((), (), s32[]{:S(2)}) async-start(), calls=%async_computation.3 | async-start | bytes 1048576 | tf_op jit(solution)/shard_map/psum | solution.py:9
  16.7 7.0 slice-start
  33.2 103.4 %copy-start.1 = (f32[128,2048]{1,0:T(8,128)S(1)}, f32[128,2048]{1,0:T(8,128)}, u32[]{:S(2)}) copy-start(f32[128,2048]{1,0:T(8,128)} %param.13) | copy-start | bytes 3145732
  451.5 54.4 %all-gather.7.cloned.1.call-start = ((), (), s32[]{:S(2)}) async-start(), calls=%async_computation.5 | async-start | bytes 2359296 | tf_op jit(solution)/shard_map/all_gather | solution.py:50
  452.1 159.6 %all-gather.5.cloned.1.call-start = ((), (), s32[]{:S(2)}) async-start(), calls=%async_computation.4 | async-start | bytes 20971520 | tf_op jit(solution)/shard_map/all_gather | solution.py:53
  502.8 0.9 copy-start.7
  502.8 1.1 copy-start.8
  502.8 187.5 %all-gather.9.cloned.1.call-start = ((), (), s32[]{:S(2)}) async-start(), calls=%async_computation.6 | async-start | bytes 2359296 | tf_op jit(solution)/shard_map/all_gather | solution.py:65
  694.2 29.2 %all-to-all-start = ((bf16[128,4,2048]{2,0,1:T(8,128)(2,1)}), bf16[128,4,2048]{2,0,1:T(8,128)(2,1)S(1)}, u32[]{:S(2)}, u32[]{:S(2)}) async-start(bf16[128,4,2048]{2,0,1:T(8,128)(2,1)} %copy.39), calls=%async_computation | async-start | bytes 4194304 | tf_op jit(solution)/shard_map/all_to_all | solution.py:68
  697.9 102.3 %reduce-scatter.2.cloned.1.call-start = ((), (), s32[]{:S(2)}) async-start(), calls=%async_computation.7 | async-start | bytes 9175040 | tf_op jit(solution)/shard_map/reduce_scatter | solution.py:70
  800.2 96.4 %copy-start = (f32[128,3584]{1,0:T(8,128)S(1)}, f32[128,3584]{1,0:T(8,128)}, u32[]{:S(2)}) copy-start(f32[128,3584]{1,0:T(8,128)} %reduce-scatter.2.cloned.1.call-done) | copy-start | bytes 5505028
  802.1 14.9 %collective-permute-start = (bf16[128,1792]{1,0:T(8,128)(2,1)S(1)}, bf16[128,1792]{1,0:T(8,128)(2,1)S(1)}, u32[]{:S(2)}, u32[]{:S(2)}) collective-permute-start(bf16[128,1792]{1,0:T(8,128)(2,1)S(1)} %fusion.9), channel_id=1, source_target_pairs={{0,1},{1,2},{2,3},{3,4},{4,5},{5,6},{6,7},{7,0},{8,9},{9,10},{10,1... | collective-permute-start | bytes 1376264 | tf_op jit(solution)/shard_map/ppermute | solution.py:81
  816.9 13.9 %collective-permute-start.1 = (bf16[128,1792]{1,0:T(8,128)(2,1)S(1)}, bf16[128,1792]{1,0:T(8,128)(2,1)S(1)}, u32[]{:S(2)}, u32[]{:S(2)}) collective-permute-start(bf16[128,1792]{1,0:T(8,128)(2,1)S(1)} %collective-permute-done), channel_id=1, source_target_pairs={{0,1},{1,2},{2,3},{3,4},{4,5},{5,6},{6,7},{7,0},{8,9},{9,10},{10,1... | collective-permute-start | bytes 1376264 | tf_op jit(solution)/shard_map/ppermute | solution.py:81
  830.9 13.1 %collective-permute-start.2 = (bf16[128,1792]{1,0:T(8,128)(2,1)S(1)}, bf16[128,1792]{1,0:T(8,128)(2,1)S(1)}, u32[]{:S(2)}, u32[]{:S(2)}) collective-permute-start(bf16[128,1792]{1,0:T(8,128)(2,1)S(1)} %collective-permute-done.1), channel_id=1, source_target_pairs={{0,1},{1,2},{2,3},{3,4},{4,5},{5,6},{6,7},{7,0},{8,9},{9,10},{10,1... | collective-permute-start | bytes 1376264 | tf_op jit(solution)/shard_map/ppermute | solution.py:81
  844.0 12.2 %collective-permute-start.3 = (bf16[128,1792]{1,0:T(8,128)(2,1)S(1)}, bf16[128,1792]{1,0:T(8,128)(2,1)S(1)}, u32[]{:S(2)}, u32[]{:S(2)}) collective-permute-start(bf16[128,1792]{1,0:T(8,128)(2,1)S(1)} %collective-permute-done.2), channel_id=1, source_target_pairs={{0,1},{1,2},{2,3},{3,4},{4,5},{5,6},{6,7},{7,0},{8,9},{9,10},{10,1... | collective-permute-start | bytes 1376264 | tf_op jit(solution)/shard_map/ppermute | solution.py:81
  856.2 0.8 copy-start.3
  857.0 11.4 %collective-permute-start.4 = (bf16[128,1792]{1,0:T(8,128)(2,1)S(1)}, bf16[128,1792]{1,0:T(8,128)(2,1)S(1)}, u32[]{:S(2)}, u32[]{:S(2)}) collective-permute-start(bf16[128,1792]{1,0:T(8,128)(2,1)S(1)} %collective-permute-done.3), channel_id=1, source_target_pairs={{0,1},{1,2},{2,3},{3,4},{4,5},{5,6},{6,7},{7,0},{8,9},{9,10},{10,1... | collective-permute-start | bytes 1376264 | tf_op jit(solution)/shard_map/ppermute | solution.py:81
  868.3 0.8 copy-start.5
  869.1 11.4 %collective-permute-start.5 = (bf16[128,1792]{1,0:T(8,128)(2,1)S(1)}, bf16[128,1792]{1,0:T(8,128)(2,1)}, u32[]{:S(2)}, u32[]{:S(2)}) collective-permute-start(bf16[128,1792]{1,0:T(8,128)(2,1)S(1)} %collective-permute-done.4), channel_id=1, source_target_pairs={{0,1},{1,2},{2,3},{3,4},{4,5},{5,6},{6,7},{7,0},{8,9},{9,10},{10,1... | collective-permute-start | bytes 1376264 | tf_op jit(solution)/shard_map/ppermute | solution.py:81
  880.5 11.5 %collective-permute-start.6 = (bf16[128,1792]{1,0:T(8,128)(2,1)}, bf16[128,1792]{1,0:T(8,128)(2,1)}, u32[]{:S(2)}, u32[]{:S(2)}) collective-permute-start(bf16[128,1792]{1,0:T(8,128)(2,1)} %collective-permute-done.5), channel_id=1, source_target_pairs={{0,1},{1,2},{2,3},{3,4},{4,5},{5,6},{6,7},{7,0},{8,9},{9,10},{10,1... | collective-permute-start | bytes 1376264 | tf_op jit(solution)/shard_map/ppermute | solution.py:81
  894.1 4.8 copy-start.6
  895.3 3.7 copy-start.4
  899.5 3.1 copy-start.2
  911.6 57.2 %all-to-all-start.1 = ((bf16[128,4,3584]{0,2,1:T(8,128)(2,1)}), bf16[128,4,3584]{0,2,1:T(8,128)(2,1)}, u32[]{:S(2)}, u32[]{:S(2)}) async-start(bf16[128,4,3584]{0,2,1:T(8,128)(2,1)} %bitcast.76), calls=%async_computation.2 | async-start | bytes 7340032 | tf_op jit(solution)/shard_map/all_to_all | solution.py:91
  916.3 58.4 %all-gather.11.cloned.1.call-start = ((), (), s32[]{:S(2)}) async-start(), calls=%async_computation.8 | async-start | bytes 2293760 | tf_op jit(solution)/shard_map/all_gather | solution.py:92
Sparse Core Ops, SparseCore 0:
  451.6 36.1 all-reduce.1
  736.5 63.6 reduce-scatter.1
  918.8 28.6 all-gather.10
Sparse Core Ops, SparseCore 1:
  454.2 51.6 all-gather.6
  507.3 104.3 all-gather.4
  645.0 45.3 all-gather.8
